TPU v7x, 32 devices: a whole 2x2x4 slice. The times are simulated.
32 devices in a mesh: beam: 8 (over y, x, core), grp: 4 (over z).
Axes of the slice: x: 2, y: 2, z: 4, core: 2. Of those that a mesh axis runs over, the one named last changes fastest.
Arguments:
- beam_data: bfloat16 [2, 4096, 256], P(None, 'beam', 'grp'), may hold values from -6 to 6
- window_count: int32 [32], P(('beam', 'grp')), may hold values from 1 to 8
- slot_owner: int32 [32, 8, 1], P(('beam', 'grp')), may hold values from 0 to 7; in each aligned block of 8 rows (0 to 7, 8 to 15, ..., all dimensions but the last counted through in order) at most 2 rows name the same one
- slot_window: int32 [32, 8], P(('beam', 'grp')), may hold values from 0 to 3
- grid_index: int32 [32, 4096], P(('beam', 'grp')), may hold values from 0 to 4095
Outputs:
- spectrum: float32 [32, 4096], P(('beam', 'grp'))
Inputs may be any that keep to these rules, and one draw needn't show every extreme that they name: a user's slots 0 to window_count - 1 are live. `slot_owner`: among the 8 slots of the users of one device no owner is named more than 2 times, a bound that some block reaches.
All inputs are finite; a program needn't handle non-finite values.
Results may differ from a plain program's by a relative error of at most 0.0003.
Values may be sent and summed in bfloat16 or wider, within the bound.
A program may use at most 64 MiB of HBM per device.

v0:
```python
import functools
import math

import jax
import jax.numpy as jnp
from jax import lax
from jax.experimental import pallas as pl
from jax.experimental.pallas import tpu as pltpu
from jax.sharding import PartitionSpec as P

WIN_BEAMS = 128
NOISE_DIM = 64
SNAPS = 256
OVERSAMPLE = 32
ITERS = 8

MESH = pl.DeviceIdType.MESH
highest = lax.Precision.HIGHEST
shift_factor = 1.05
spectral_floor = 0.05
CHUNK = 512
FAST_LOW = 1.0 / 64
FAST_STEPS = 8


def cubic_schedule(low, steps):
    pairs = []
    for _ in range(steps):
        form = 1.0 + low + low * low
        scale = 3.0 * math.sqrt(3.0) / (2.0 * form**1.5)
        pairs.append((form * scale, scale))
        low = min((low + low * low) * scale, 1.0)
    return pairs


def dot(left, right):
    return jnp.dot(left, right, precision=highest, preferred_element_type=jnp.float32)


def dot_tn(left, right):
    return lax.dot_general(
        left,
        right,
        (((0,), (0,)), ((), ())),
        precision=highest,
        preferred_element_type=jnp.float32,
    )


def dot_nt(left, right):
    return lax.dot_general(
        left, right, (((1,), (1,)), ((), ())), preferred_element_type=jnp.float32
    )


def exchange_kernel(
    n_beam,
    n_grp,
    users,
    windows,
    x_ref,
    weight_ref,
    out_ref,
    held,
    weights_in,
    outgoing,
    incoming,
    x_send,
    x_recv,
    w_send,
    w_recv,
    o_send,
    o_recv,
):
    beam = lax.axis_index("beam")
    grp = lax.axis_index("grp")
    width = WIN_BEAMS

    barrier = pltpu.get_barrier_semaphore()
    for j in range(1, n_grp):
        pl.semaphore_signal(
            barrier, inc=1, device_id=(beam, lax.rem(grp + j, n_grp)), device_id_type=MESH
        )
    for j in range(1, n_beam):
        pl.semaphore_signal(
            barrier, inc=1, device_id=(lax.rem(beam + j, n_beam), grp), device_id_type=MESH
        )
    pl.semaphore_wait(barrier, n_grp + n_beam - 2)

    x_copies = []
    for j in range(1, n_grp):
        copy = pltpu.make_async_remote_copy(
            src_ref=x_ref,
            dst_ref=held.at[j - 1],
            send_sem=x_send.at[j - 1],
            recv_sem=x_recv.at[j - 1],
            device_id=(beam, lax.rem(grp + j, n_grp)),
            device_id_type=MESH,
        )
        copy.start()
        x_copies.append(copy)
    w_copies = []
    for j in range(1, n_beam):
        owner = lax.rem(beam + j, n_beam)
        copy = pltpu.make_async_remote_copy(
            src_ref=weight_ref.at[owner],
            dst_ref=weights_in.at[j - 1],
            send_sem=w_send.at[j - 1],
            recv_sem=w_recv.at[j - 1],
            device_id=(owner, grp),
            device_id_type=MESH,
        )
        copy.start()
        w_copies.append(copy)

    row = lax.broadcasted_iota(jnp.int32, (width, width), 0)
    col = lax.broadcasted_iota(jnp.int32, (width, width), 1)
    lanes = x_ref.shape[1]
    from_lane = lax.broadcasted_iota(jnp.int32, (lanes, lanes), 0)
    to_lane = lax.broadcasted_iota(jnp.int32, (lanes, lanes), 1)
    turn = jnp.where(
        from_lane == to_lane + lanes // 2, -1.0, jnp.where(to_lane == from_lane + lanes // 2, 1.0, 0.0)
    ).astype(jnp.bfloat16)
    same = [None] * windows
    cross = [None] * windows
    for j in range(n_grp):
        if j > 0:
            x_copies[j - 1].wait_recv()
        source = x_ref if j == 0 else held.at[j - 1]
        for w in range(windows):
            piece = source[w * width : (w + 1) * width, :]
            turned = jnp.dot(piece, turn, preferred_element_type=jnp.float32).astype(jnp.bfloat16)
            part_same = dot_nt(piece, piece)
            part_cross = dot_nt(piece, turned)
            same[w] = part_same if j == 0 else same[w] + part_same
            cross[w] = part_cross if j == 0 else cross[w] + part_cross
    packed = [jnp.where(col >= row, same[w], cross[w]) for w in range(windows)]

    def mixed(weights):
        totals = []
        for u in range(users):
            total = packed[0] * weights[u, 0:1, :]
            for w in range(1, windows):
                total = total + packed[w] * weights[u, w : w + 1, :]
            totals.append(total)
        return totals

    o_copies = []
    for j in range(1, n_beam):
        w_copies[j - 1].wait_recv()
        totals = mixed(weights_in[j - 1])
        for u in range(users):
            outgoing[j - 1, u] = totals[u]
    for j in range(1, n_beam):
        copy = pltpu.make_async_remote_copy(
            src_ref=outgoing.at[j - 1],
            dst_ref=incoming.at[j - 1],
            send_sem=o_send.at[j - 1],
            recv_sem=o_recv.at[j - 1],
            device_id=(lax.rem(beam + n_beam - j, n_beam), grp),
            device_id_type=MESH,
        )
        copy.start()
        o_copies.append(copy)
    totals = mixed(weight_ref[beam])
    for j in range(1, n_beam):
        o_copies[j - 1].wait_recv()
        for u in range(users):
            totals[u] = totals[u] + incoming[j - 1, u]
    for u in range(users):
        out_ref[u] = totals[u]
    for copy in x_copies + w_copies + o_copies:
        copy.wait_send()


def exchange(x_local, weights, n_beam, n_grp):
    rows = x_local.shape[0]
    users, padded = weights.shape[1], weights.shape[2]
    windows = rows // WIN_BEAMS
    sums = (users, WIN_BEAMS, WIN_BEAMS)
    return pl.pallas_call(
        functools.partial(exchange_kernel, n_beam, n_grp, users, windows),
        out_shape=jax.ShapeDtypeStruct(sums, jnp.float32),
        in_specs=[pl.BlockSpec(memory_space=pltpu.VMEM)] * 2,
        out_specs=pl.BlockSpec(memory_space=pltpu.VMEM),
        scratch_shapes=[
            pltpu.VMEM((n_grp - 1,) + x_local.shape, jnp.bfloat16),
            pltpu.VMEM((n_beam - 1, users, padded, WIN_BEAMS), jnp.float32),
            pltpu.VMEM((n_beam - 1,) + sums, jnp.float32),
            pltpu.VMEM((n_beam - 1,) + sums, jnp.float32),
            pltpu.SemaphoreType.DMA((n_grp - 1,)),
            pltpu.SemaphoreType.DMA((n_grp - 1,)),
            pltpu.SemaphoreType.DMA((n_beam - 1,)),
            pltpu.SemaphoreType.DMA((n_beam - 1,)),
            pltpu.SemaphoreType.DMA((n_beam - 1,)),
            pltpu.SemaphoreType.DMA((n_beam - 1,)),
        ],
        compiler_params=pltpu.CompilerParams(collective_id=0, has_side_effects=True),
    )(x_local, weights)


def spectrum_kernel(beams_total, sum_ref, count_ref, grid_ref, out_ref, basis_ref):
    width, dim = WIN_BEAMS, NOISE_DIM
    packed = sum_ref[0]
    flipped = packed.T
    row = lax.broadcasted_iota(jnp.int32, (width, width), 0)
    col = lax.broadcasted_iota(jnp.int32, (width, width), 1)
    count = count_ref[pl.program_id(0)].astype(jnp.float32)
    inverse_count = 1.0 / (jnp.zeros((1, width), jnp.float32) + count * SNAPS)
    real_sum = jnp.where(col >= row, packed, flipped) * inverse_count
    imag_sum = jnp.where(col < row, packed, jnp.where(col > row, -flipped, 0.0)) * inverse_count
    covariance = jnp.concatenate(
        [
            jnp.concatenate([real_sum, -imag_sum], axis=1),
            jnp.concatenate([imag_sum, real_sum], axis=1),
        ],
        axis=0,
    )
    square = dot(covariance, covariance)
    fourth = dot(square, square[:, :width])
    energy = 2.0 * jnp.sum(fourth * fourth, keepdims=True)
    shift_value = shift_factor * jnp.sqrt(jnp.sqrt(jnp.sqrt(energy)))
    row2 = lax.broadcasted_iota(jnp.int32, (2 * width, 2 * width), 0)
    col2 = lax.broadcasted_iota(jnp.int32, (2 * width, 2 * width), 1)
    shifted = jnp.where(row2 == col2, 1.0, 0.0) - covariance * (1.0 / shift_value)

    def chosen(matrix):
        return jnp.concatenate([matrix[:, :dim], matrix[:, width : width + dim]], axis=1)

    eye = jnp.where(row == col, 1.0, 0.0)

    def cubic(block, pairs):
        for a, b in pairs:
            gram = dot_tn(block, block)
            block = dot(block, a * eye - b * gram)
        return block

    second = dot(shifted, shifted)
    power = dot(second, second)
    block = dot(power, chosen(power))
    gram = dot_tn(block, block)
    scale = lax.rsqrt(jnp.sqrt(jnp.sum(gram * gram, keepdims=True)))
    block = cubic(block * scale, cubic_schedule(FAST_LOW, FAST_STEPS))
    basis_ref[...] = block
    miss = dot_tn(block, block) - eye
    well = jnp.sum(miss * miss) < 1e-9

    @pl.when(jnp.logical_not(well))
    def _():
        start = jnp.where(
            (row2 == col2)[:, :width] & (col < dim)[:1], 1.0, 0.0
        ) + jnp.where(row2[:, :width] == col2[:, :width] + (width - dim), 1.0, 0.0) * jnp.where(
            col2[:, :width] >= dim, 1.0, 0.0
        )
        basis_ref[...] = start
        pairs = cubic_schedule(0.0132, 5)

        @pl.loop(0, ITERS // 2)
        def _(_):
            basis_ref[...] = cubic(dot(second, basis_ref[...]), pairs)

        basis_ref[...] = cubic(basis_ref[...], [(1.5, 0.5)] * 4)

    theta = row.astype(jnp.float32) * (math.pi / beams_total)
    weight = basis_ref[:width, :] * jnp.cos(theta) + basis_ref[width:, :] * jnp.sin(theta)
    weight = weight.T
    grid_points = grid_ref.shape[-1]
    chunk = math.gcd(CHUNK, grid_points)
    beam_at = lax.broadcasted_iota(jnp.int32, (width, chunk), 0) * OVERSAMPLE
    for at in range(0, grid_points, chunk):
        offset = (grid_ref[0, :, at : at + chunk] - beam_at).astype(jnp.float32) + 0.5
        angle = offset * (math.pi / (OVERSAMPLE * beams_total))
        sq = angle * angle
        sine = offset * (
            1.0 + sq * (-1.0 / 6 + sq * (1.0 / 120 + sq * (-1.0 / 5040 + sq * (1.0 / 362880))))
        )
        steer = OVERSAMPLE / sine
        projected = dot(weight, steer)
        leakage = jnp.sum(projected * projected, axis=0, keepdims=True) / jnp.sum(
            steer * steer, axis=0, keepdims=True
        )
        out_ref[0, :, at : at + chunk] = 1.0 / (leakage + spectral_floor)


def finish_users(sums, counts, grid_index, beams_total):
    users, points = grid_index.shape
    width = WIN_BEAMS
    out = pl.pallas_call(
        functools.partial(spectrum_kernel, beams_total),
        grid=(users,),
        out_shape=jax.ShapeDtypeStruct((users, 1, points), jnp.float32),
        in_specs=[
            pl.BlockSpec((1, width, width), lambda u: (u, 0, 0)),
            pl.BlockSpec(memory_space=pltpu.SMEM),
            pl.BlockSpec((1, 1, points), lambda u: (u, 0, 0)),
        ],
        out_specs=pl.BlockSpec((1, 1, points), lambda u: (u, 0, 0)),
        scratch_shapes=[pltpu.VMEM((2 * width, 2 * NOISE_DIM), jnp.float32)],
    )(sums, counts, grid_index.reshape(users, 1, points))
    return out.reshape(users, points)


def local(n_beam, n_grp, beam_data, window_count, slot_owner, slot_window, grid_index):
    slot_count = slot_window.shape[1]
    windows = beam_data.shape[1] // WIN_BEAMS
    padded = -(-windows // 8) * 8
    beams_total = beam_data.shape[1] * n_beam
    x_local = jnp.concatenate([beam_data[0], beam_data[1]], axis=-1)
    live = jnp.arange(slot_count, dtype=jnp.int32)[None, :] < window_count[:, None]
    named = jnp.where(live, slot_owner[:, :, 0] * padded + slot_window, -1)
    slots = jnp.arange(n_beam * padded, dtype=jnp.int32).reshape(n_beam, 1, padded)
    hits = (named[None, :, None, :] == slots[..., None]).astype(jnp.float32)
    weights = jnp.broadcast_to(
        jnp.sum(hits, axis=-1)[..., None], (n_beam, window_count.shape[0], padded, WIN_BEAMS)
    )
    sums = exchange(x_local, weights, n_beam, n_grp)
    return finish_users(sums, window_count, grid_index, beams_total)


def solution(mesh):
    placed = (
        P(None, "beam", "grp"),
        P(("beam", "grp")),
        P(("beam", "grp"), None, None),
        P(("beam", "grp"), None),
        P(("beam", "grp"), None),
    )
    return jax.shard_map(
        functools.partial(local, mesh.shape["beam"], mesh.shape["grp"]),
        mesh=mesh,
        in_specs=placed,
        out_specs=P(("beam", "grp"), None),
        check_vma=False,
    )
```

profile of v0, /device:TPU:0, one launch (start us, length us, event | category | flops | bytes accessed | tf_op | source)
XLA Modules:
  0.0 44.3 jit_solution(8827535513721945420)
XLA Ops:
  0.0 0.9 %fusion.1 = (bf16[1,512,64]{1,2,0:T(8,128)(2,1)S(1)}, bf16[1,512,64]{1,2,0:T(8,128)(2,1)S(1)}) fusion(bf16[2,512,64]{1,2,0:T(8,128)(2,1)} %param.5), kind=kLoop, calls=%fused_computation.6 | loop fusion | bytes 262144 | tf_op jit(solution)/shard_map/slice | solution.py:308
  0.9 0.1 copy.10
  1.0 0.1 copy.11
  1.1 0.8 %pad_maximum_fusion.x_ref = bf16[512,128]{1,0:T(8,128)(2,1)} fusion(bf16[512,64]{1,0:T(8,128)(2,1)S(1)} %bitcast.13, bf16[512,64]{1,0:T(8,128)(2,1)S(1)} %bitcast.12), kind=kLoop, calls=%fused_computation | loop fusion | flops 262144 | bytes 262144 | tf_op jit(solution)/shard_map/concatenate | solution.py:308
  2.6 0.0 copy-start
  2.6 0.0 copy-start.1
  2.6 0.6 %copy-done = s32[1,8]{1,0:T(1,128)S(1)} copy-done((s32[1,8]{1,0:T(1,128)S(1)}, s32[1,8]{1,0:T(1,128)}, u32[]{:S(2)}) %copy-start) | copy-done | bytes 56
  3.2 0.0 copy-done.1
  3.2 0.2 convert_reduce_fusion
  3.4 0.7 %broadcast_in_dim.7.weight_ref = f32[8,1,8,128]{3,2,1,0:T(8,128)} broadcast(f32[8,8]{1,0:T(8,128)S(1)} %convert_reduce_fusion), dimensions={0,2} | broadcast | bytes 33024 | tf_op jit(solution)/shard_map/broadcast_in_dim | solution.py:313
  4.1 25.9 %shard_map.55.sum_ref = f32[1,128,128]{2,1,0:T(8,128)} custom-call(bf16[512,128]{1,0:T(8,128)(2,1)} %pad_maximum_fusion.x_ref, f32[8,1,8,128]{3,2,1,0:T(8,128)} %broadcast_in_dim.7.weight_ref), custom_call_target="tpu_custom_call" | custom-call | tf_op jit(solution)/shard_map/pallas_call | solution.py:181
  30.0 14.2 %shard_map.56 = f32[1,1,4096]{2,1,0:T(1,128)} custom-call(f32[1,128,128]{2,1,0:T(8,128)} %shard_map.55.sum_ref, s32[1]{0:T(128)} %copy.12.count_ref, s32[1,1,4096]{2,1,0:T(1,128)} %bitcast.14), custom_call_target="tpu_custom_call" | custom-call | tf_op jit(solution)/shard_map/pallas_call | solution.py:288
  (2 shorter events, 0.0 us)
Async XLA Ops:
  2.6 0.7 %copy-start = (s32[1,8]{1,0:T(1,128)S(1)}, s32[1,8]{1,0:T(1,128)}, u32[]{:S(2)}) copy-start(s32[1,8]{1,0:T(1,128)} %param.8) | copy-start | bytes 100
  2.6 0.7 %copy-start.1 = (s32[1,8,1]{1,2,0:T(1,128)S(1)}, s32[1,8,1]{1,2,0:T(1,128)}, u32[]{:S(2)}) copy-start(s32[1,8,1]{1,2,0:T(1,128)} %param.7) | copy-start | bytes 100
where the time goes:
time: 44.5 us; the launch traced here: 44.3 us
  Pallas kernels  40.2 us (90%)
  local copies, waits for them, and re-layouts  2.47 us (6%)
  other arithmetic  0.93 us (2%)
  between operations  0.7 us (2%)
    pallas_call x1, Pallas kernels, exchange(): pl.pallas_call(functools.partial(exchange_kernel, n_beam, n_grp, users, w...  25.9 us
    pallas_call x1, Pallas kernels, finish_users(): pl.pallas_call(functools.partial(spectrum_kernel, beams_total), grid=(use...  14.2 us
    unnamed x6, local copies, waits for them, and re-layouts  0.9 us

commit v1 on v0

v1 whole, which is shorter than its diff:
```python
import functools
import math

import jax
import jax.numpy as jnp
from jax import lax
from jax.experimental import pallas as pl
from jax.experimental.pallas import tpu as pltpu
from jax.sharding import PartitionSpec as P

WIN_BEAMS = 128
NOISE_DIM = 64
SNAPS = 256
OVERSAMPLE = 32
ITERS = 8

MESH = pl.DeviceIdType.MESH
highest = lax.Precision.HIGHEST
shift_factor = 1.05
spectral_floor = 0.05
CHUNK = 512
FAST_LOW = 1.0 / 36
FAST_STEPS = 7
FAST_COARSE = 4
FAST_MISS = 3e-8


def cubic_schedule(low, steps):
    pairs = []
    for _ in range(steps):
        form = 1.0 + low + low * low
        scale = 3.0 * math.sqrt(3.0) / (2.0 * form**1.5)
        pairs.append((form * scale, scale))
        low = min((low + low * low) * scale, 1.0)
    return pairs


def dot(left, right):
    return jnp.dot(left, right, precision=highest, preferred_element_type=jnp.float32)


def dot_tn(left, right):
    return lax.dot_general(
        left,
        right,
        (((0,), (0,)), ((), ())),
        precision=highest,
        preferred_element_type=jnp.float32,
    )


def halves(matrix):
    high = matrix.astype(jnp.bfloat16)
    return high, (matrix - high.astype(jnp.float32)).astype(jnp.bfloat16)


def plain(left, right, contract=1):
    return lax.dot_general(
        left,
        right,
        (((contract,), (0,)), ((), ())),
        preferred_element_type=jnp.float32,
    )


def dot3(left, right, contract=1):
    (left_high, left_low), (right_high, right_low) = left, right
    return plain(left_high, right_high, contract) + (
        plain(left_high, right_low, contract) + plain(left_low, right_high, contract)
    )


def dot_nt(left, right):
    return lax.dot_general(
        left, right, (((1,), (1,)), ((), ())), preferred_element_type=jnp.float32
    )


def exchange_kernel(
    n_beam,
    n_grp,
    windows,
    beams_total,
    data_ref,
    count_ref,
    owner_ref,
    window_ref,
    grid_ref,
    out_ref,
    high_ref,
    low_ref,
    norm_ref,
    held,
    weights,
    weights_in,
    outgoing,
    incoming,
    same,
    cross,
    x_send,
    x_recv,
    w_send,
    w_recv,
    o_send,
    o_recv,
):
    beam = lax.axis_index("beam")
    grp = lax.axis_index("grp")
    width = WIN_BEAMS
    users, slots = window_ref.shape
    padded = weights.shape[2]

    barrier = pltpu.get_barrier_semaphore()
    has_right = grp < n_grp - 1
    has_left = grp > 0

    @pl.when(has_right)
    def _():
        pl.semaphore_signal(barrier, inc=1, device_id=(beam, grp + 1), device_id_type=MESH)

    @pl.when(has_left)
    def _():
        pl.semaphore_signal(barrier, inc=1, device_id=(beam, grp - 1), device_id_type=MESH)

    for j in range(1, n_beam):
        pl.semaphore_signal(
            barrier, inc=1, device_id=(lax.rem(beam + j, n_beam), grp), device_id_type=MESH
        )

    held[grp] = jnp.concatenate([data_ref[0], data_ref[1]], axis=1)
    entry = lax.broadcasted_iota(jnp.int32, (n_beam, padded, width), 0) * padded + (
        lax.broadcasted_iota(jnp.int32, (n_beam, padded, width), 1)
    )
    for u in range(users):
        total = jnp.zeros((n_beam, padded, width), jnp.float32)
        for k in range(slots):
            named = owner_ref[u, k] * padded + window_ref[u, k]
            live = (k < count_ref[u]).astype(jnp.float32)
            total = total + jnp.where(entry == named, 1.0, 0.0) * live
        weights[:, u] = total

    pl.semaphore_wait(
        barrier, has_right.astype(jnp.int32) + has_left.astype(jnp.int32) + n_beam - 1
    )

    def hop(way, step, w):
        source = grp - (step - 1) if way == 0 else grp + (step - 1)
        rows = pl.ds(w * width, width)
        return pltpu.make_async_remote_copy(
            src_ref=held.at[source, rows],
            dst_ref=held.at[source, rows],
            send_sem=x_send.at[way, step - 1, w],
            recv_sem=x_recv.at[way, step - 1, w],
            device_id=(beam, grp + 1 if way == 0 else grp - 1),
            device_id_type=MESH,
        )

    def arrival(way, step, w):
        source = grp - step if way == 0 else grp + step
        rows = pl.ds(w * width, width)
        return pltpu.make_async_remote_copy(
            src_ref=held.at[source, rows],
            dst_ref=held.at[source, rows],
            send_sem=x_send.at[way, step - 1, w],
            recv_sem=x_recv.at[way, step - 1, w],
            device_id=(beam, grp - 1 if way == 0 else grp + 1),
            device_id_type=MESH,
        )

    def sends(way, step):
        if way == 0:
            return has_right & (grp >= step - 1)
        return has_left & (grp + step - 1 < n_grp)

    def receives(way, step):
        return grp >= step if way == 0 else grp + step < n_grp

    for way in range(2):

        @pl.when(sends(way, 1))
        def _():
            for w in range(windows):
                hop(way, 1, w).start()

    w_copies = []
    for j in range(1, n_beam):
        owner = lax.rem(beam + j, n_beam)
        copy = pltpu.make_async_remote_copy(
            src_ref=weights.at[owner],
            dst_ref=weights_in.at[j - 1],
            send_sem=w_send.at[j - 1],
            recv_sem=w_recv.at[j - 1],
            device_id=(owner, grp),
            device_id_type=MESH,
        )
        copy.start()
        w_copies.append(copy)

    row = lax.broadcasted_iota(jnp.int32, (width, width), 0)
    col = lax.broadcasted_iota(jnp.int32, (width, width), 1)
    lanes = held.shape[2]
    from_lane = lax.broadcasted_iota(jnp.int32, (lanes, lanes), 0)
    to_lane = lax.broadcasted_iota(jnp.int32, (lanes, lanes), 1)
    turn = jnp.where(
        from_lane == to_lane + lanes // 2, -1.0, jnp.where(to_lane == from_lane + lanes // 2, 1.0, 0.0)
    ).astype(jnp.bfloat16)

    def grams(source, w):
        piece = held[source, w * width : (w + 1) * width, :]
        turned = plain(piece, turn).astype(jnp.bfloat16)
        return dot_nt(piece, piece), dot_nt(piece, turned)

    for w in range(windows):
        same[w], cross[w] = grams(grp, w)
    for step in range(1, n_grp):
        for w in range(windows):
            for way in range(2):

                @pl.when(receives(way, step))
                def _():
                    arrival(way, step, w).wait_recv()

                if step < n_grp - 1:

                    @pl.when(sends(way, step + 1))
                    def _():
                        hop(way, step + 1, w).start()

        for way in range(2):

            @pl.when(receives(way, step))
            def _():
                source = grp - step if way == 0 else grp + step
                for w in range(windows):
                    more_same, more_cross = grams(source, w)
                    same[w] += more_same
                    cross[w] += more_cross

    for w in range(windows):
        same[w] = jnp.where(col >= row, same[w], cross[w])

    def mixed(shares, u):
        total = same[0] * shares[u, 0:1, :]
        for w in range(1, windows):
            total = total + same[w] * shares[u, w : w + 1, :]
        return total

    o_copies = []
    for j in range(1, n_beam):
        o_copies.append(
            pltpu.make_async_remote_copy(
                src_ref=outgoing.at[j - 1],
                dst_ref=incoming.at[j - 1],
                send_sem=o_send.at[j - 1],
                recv_sem=o_recv.at[j - 1],
                device_id=(lax.rem(beam + n_beam - j, n_beam), grp),
                device_id_type=MESH,
            )
        )
    for j in range(1, n_beam):
        w_copies[j - 1].wait_recv()
        for u in range(users):
            outgoing[j - 1, u] = mixed(weights_in[j - 1], u)
        if j > 1:
            o_copies[j - 2].start()
    for u in range(users):
        out_ref[u] = mixed(weights[beam], u)
    o_copies[-1].start()

    points = grid_ref.shape[-1]
    chunk = math.gcd(CHUNK, points)
    beam_at = lax.broadcasted_iota(jnp.int32, (width, chunk), 0) * OVERSAMPLE
    for u in range(users):

        @pl.loop(0, points // chunk)
        def _(at):
            span = pl.ds(pl.multiple_of(at * chunk, chunk), chunk)
            offset = (grid_ref[u, :, span] - beam_at).astype(jnp.float32) + 0.5
            angle = offset * (math.pi / (OVERSAMPLE * beams_total))
            sq = angle * angle
            sine = offset * (
                1.0 + sq * (-1.0 / 6 + sq * (1.0 / 120 + sq * (-1.0 / 5040 + sq * (1.0 / 362880))))
            )
            steer = OVERSAMPLE / sine
            high_ref[u, :, span], low_ref[u, :, span] = halves(steer)
            norm_ref[u, :, span] = jnp.sum(steer * steer, axis=0, keepdims=True)

    for j in range(1, n_beam):
        o_copies[j - 1].wait_recv()
        for u in range(users):
            out_ref[u] += incoming[j - 1, u]
    for copy in w_copies + o_copies:
        copy.wait_send()
    for way in range(2):
        for step in range(1, n_grp):

            @pl.when(sends(way, step))
            def _():
                for w in range(windows):
                    hop(way, step, w).wait_send()


def exchange(beam_data, counts, owners, slot_window, grid_index, n_beam, n_grp):
    rows = beam_data.shape[1]
    windows = rows // WIN_BEAMS
    padded = -(-windows // 8) * 8
    users, points = grid_index.shape[0], grid_index.shape[2]
    width = WIN_BEAMS
    sums = (users, width, width)
    shares = (users, padded, width)
    vmem = pl.BlockSpec(memory_space=pltpu.VMEM)
    smem = pl.BlockSpec(memory_space=pltpu.SMEM)
    return pl.pallas_call(
        functools.partial(exchange_kernel, n_beam, n_grp, windows, rows * n_beam),
        out_shape=[
            jax.ShapeDtypeStruct(sums, jnp.float32),
            jax.ShapeDtypeStruct((users, width, points), jnp.bfloat16),
            jax.ShapeDtypeStruct((users, width, points), jnp.bfloat16),
            jax.ShapeDtypeStruct((users, 1, points), jnp.float32),
        ],
        in_specs=[vmem, smem, smem, smem, vmem],
        out_specs=[vmem] * 4,
        scratch_shapes=[
            pltpu.VMEM((n_grp, rows, 2 * beam_data.shape[2]), jnp.bfloat16),
            pltpu.VMEM((n_beam,) + shares, jnp.float32),
            pltpu.VMEM((n_beam - 1,) + shares, jnp.float32),
            pltpu.VMEM((n_beam - 1,) + sums, jnp.float32),
            pltpu.VMEM((n_beam - 1,) + sums, jnp.float32),
            pltpu.VMEM((windows, width, width), jnp.float32),
            pltpu.VMEM((windows, width, width), jnp.float32),
            pltpu.SemaphoreType.DMA((2, n_grp - 1, windows)),
            pltpu.SemaphoreType.DMA((2, n_grp - 1, windows)),
            pltpu.SemaphoreType.DMA((n_beam - 1,)),
            pltpu.SemaphoreType.DMA((n_beam - 1,)),
            pltpu.SemaphoreType.DMA((n_beam - 1,)),
            pltpu.SemaphoreType.DMA((n_beam - 1,)),
        ],
        compiler_params=pltpu.CompilerParams(collective_id=0, has_side_effects=True),
    )(beam_data, counts, owners, slot_window, grid_index)


def spectrum_kernel(
    beams_total, sum_ref, count_ref, high_ref, low_ref, norm_ref, out_ref, basis_ref
):
    width, dim = WIN_BEAMS, NOISE_DIM
    packed = sum_ref[0]
    flipped = packed.T
    row = lax.broadcasted_iota(jnp.int32, (width, width), 0)
    col = lax.broadcasted_iota(jnp.int32, (width, width), 1)
    count = count_ref[pl.program_id(0)].astype(jnp.float32)
    inverse_count = 1.0 / (jnp.zeros((1, width), jnp.float32) + count * SNAPS)
    real_sum = jnp.where(col >= row, packed, flipped) * inverse_count
    imag_sum = jnp.where(col < row, packed, jnp.where(col > row, -flipped, 0.0)) * inverse_count
    covariance = jnp.concatenate(
        [
            jnp.concatenate([real_sum, -imag_sum], axis=1),
            jnp.concatenate([imag_sum, real_sum], axis=1),
        ],
        axis=0,
    )
    parts = halves(covariance)
    square = halves(dot3(parts, parts))
    fourth = dot3(square, [half[:, :width] for half in square])
    energy = 2.0 * jnp.sum(fourth * fourth, keepdims=True)
    shift_value = shift_factor * jnp.sqrt(jnp.sqrt(jnp.sqrt(energy)))
    row2 = lax.broadcasted_iota(jnp.int32, (2 * width, 2 * width), 0)
    col2 = lax.broadcasted_iota(jnp.int32, (2 * width, 2 * width), 1)
    shifted = jnp.where(row2 == col2, 1.0, 0.0) - covariance * (1.0 / shift_value)

    def chosen(matrix):
        return jnp.concatenate([matrix[:, :dim], matrix[:, width : width + dim]], axis=1)

    eye = jnp.where(row == col, 1.0, 0.0)

    def cubic(block, pairs):
        for a, b in pairs:
            gram = dot_tn(block, block)
            block = dot(block, a * eye - b * gram)
        return block

    parts = halves(shifted)
    second = halves(dot3(parts, parts))
    power = dot3(second, second)
    block = dot3(halves(power), halves(chosen(power)))
    parts = halves(block)
    gram = dot3(parts, parts, 0)
    scale = 2.0**0.25 * lax.rsqrt(jnp.sqrt(jnp.sum(gram * gram, keepdims=True)))
    block, gram = block * scale, gram * (scale * scale)
    for step, (a, b) in enumerate(cubic_schedule(FAST_LOW, FAST_STEPS)):
        parts = halves(block)
        if step >= FAST_COARSE:
            gram = dot3(parts, parts, 0)
        elif step > 0:
            gram = plain(parts[0], parts[0], 0)
        block = a * block - b * dot3(parts, halves(gram))
    basis_ref[...] = block
    parts = halves(block)
    miss = dot3(parts, parts, 0) - eye
    well = jnp.sum(miss * miss) < FAST_MISS

    @pl.when(jnp.logical_not(well))
    def _():
        start = jnp.where(
            (row2 == col2)[:, :width] & (col < dim)[:1], 1.0, 0.0
        ) + jnp.where(row2[:, :width] == col2[:, :width] + (width - dim), 1.0, 0.0) * jnp.where(
            col2[:, :width] >= dim, 1.0, 0.0
        )
        basis_ref[...] = start
        second = dot(shifted, shifted)
        pairs = cubic_schedule(0.0132, 5)

        @pl.loop(0, ITERS // 2)
        def _(_):
            basis_ref[...] = cubic(dot(second, basis_ref[...]), pairs)

        basis_ref[...] = cubic(basis_ref[...], [(1.5, 0.5)] * 4)

    theta = row.astype(jnp.float32) * (math.pi / beams_total)
    weight = basis_ref[:width, :] * jnp.cos(theta) + basis_ref[width:, :] * jnp.sin(theta)
    weight = weight.T
    weight = halves(weight)
    points = norm_ref.shape[-1]
    chunk = math.gcd(CHUNK, points)
    for at in range(0, points, chunk):
        span = slice(at, at + chunk)
        projected = dot3(weight, (high_ref[0, :, span], low_ref[0, :, span]))
        leakage = jnp.sum(projected * projected, axis=0, keepdims=True) / norm_ref[0, :, span]
        out_ref[0, :, span] = 1.0 / (leakage + spectral_floor)


def finish_users(sums, counts, high, low, norm, beams_total):
    users, width, points = high.shape

    def block(*shape):
        return pl.BlockSpec((1,) + shape, lambda u: (u, 0, 0))

    return pl.pallas_call(
        functools.partial(spectrum_kernel, beams_total),
        grid=(users,),
        out_shape=jax.ShapeDtypeStruct((users, 1, points), jnp.float32),
        in_specs=[
            block(width, width),
            pl.BlockSpec(memory_space=pltpu.SMEM),
            block(width, points),
            block(width, points),
            block(1, points),
        ],
        out_specs=block(1, points),
        scratch_shapes=[pltpu.VMEM((2 * width, 2 * NOISE_DIM), jnp.float32)],
    )(sums, counts, high, low, norm).reshape(users, points)


def local(n_beam, n_grp, beam_data, window_count, slot_owner, slot_window, grid_index):
    users, points = grid_index.shape
    sums, high, low, norm = exchange(
        beam_data,
        window_count,
        slot_owner[:, :, 0],
        slot_window,
        grid_index.reshape(users, 1, points),
        n_beam,
        n_grp,
    )
    return finish_users(
        sums, window_count, high, low, norm, beam_data.shape[1] * n_beam
    )


def solution(mesh):
    placed = (
        P(None, "beam", "grp"),
        P(("beam", "grp")),
        P(("beam", "grp"), None, None),
        P(("beam", "grp"), None),
        P(("beam", "grp"), None),
    )
    return jax.shard_map(
        functools.partial(local, mesh.shape["beam"], mesh.shape["grp"]),
        mesh=mesh,
        in_specs=placed,
        out_specs=P(("beam", "grp"), None),
        check_vma=False,
    )
```

time: 44.5 us -> 37.4 us (0.84)
  Pallas kernels: 40.2 us -> 34.8 us
  other arithmetic: 0.93 us -> 0 us
  local copies, waits for them, and re-layouts: 2.47 us -> 1.78 us
    pallas_call x1, Pallas kernels: 14.2 us -> 9.02 us  [finish_users(): pl.pallas_call(functools.partial(spectrum_kernel, beams_total), grid=(use...]
    unnamed x6 -> x1, local copies, waits for them, and re-layouts: 0.9 us -> 1.78 us
    slice x1 -> x0, local copies, waits for them, and re-layouts: 0.88 us -> none  [local(): x_local = jnp.concatenate([beam_data[0], beam_data[1]], axis=-1)]
    concatenate x1 -> x0, other arithmetic: 0.77 us -> none  [local(): x_local = jnp.concatenate([beam_data[0], beam_data[1]], axis=-1)]
    broadcast_in_dim x1 -> x0, local copies, waits for them, and re-layouts: 0.69 us -> none  [local(): jnp.broadcast_to(jnp.sum(hits, axis=-1)[..., None], (n_beam, window_count...]
where the time goes in v1:
time: 37.4 us; the launch traced here: 37.3 us
  Pallas kernels  34.8 us (93%)
  local copies, waits for them, and re-layouts  1.78 us (5%)
  between operations  0.66 us (2%)
    pallas_call x1, Pallas kernels, exchange(): pl.pallas_call(functools.partial(exchange_kernel, n_beam, n_grp, windows,...  25.8 us
    pallas_call x1, Pallas kernels, finish_users(): pl.pallas_call(functools.partial(spectrum_kernel, beams_total), grid=(use...  9.02 us
    unnamed x1, local copies, waits for them, and re-layouts  1.78 us

profile of v1, /device:TPU:0, one launch (start us, length us, event | category | flops | bytes accessed | tf_op | source)
XLA Modules:
  0.0 37.3 jit_solution(6237882628159224656)
XLA Ops:
  0.7 1.8 %copy.6.data_ref = bf16[2,512,64]{2,1,0:T(8,128)(2,1)} copy(bf16[2,512,64]{1,2,0:T(8,128)(2,1)} %param.5) | data formatting | bytes 262144 | tf_op args[0]
  2.4 25.8 %shard_map.55 = (f32[1,128,128]{2,1,0:T(8,128)}, bf16[1,128,4096]{2,1,0:T(8,128)(2,1)}, bf16[1,128,4096]{2,1,0:T(8,128)(2,1)}, f32[1,1,4096]{2,1,0:T(1,128)}) custom-call(bf16[2,512,64]{2,1,0:T(8,128)(2,1)} %copy.6.data_ref, s32[1]{0:T(128)S(6)} %copy.7.count_ref, s32[1,8]{1,0:T(1,128)} %bitcast.4, s32[1,8]{1,0:T(1,128)} %window_ref.1, s32[1,1,4096]{2,1,0:T(1,128)} %bitcast.3), custom_call_target="tpu_custom_call" | custom-call | tf_op jit(solution)/shard_map/pallas_call | solution.py:313
  28.2 9.0 %shard_map.56 = f32[1,1,4096]{2,1,0:T(1,128)} custom-call(f32[1,128,128]{2,1,0:T(8,128)} %get-tuple-element.9.sum_ref, s32[1]{0:T(128)S(6)} %copy.7.count_ref, bf16[1,128,4096]{2,1,0:T(8,128)(2,1)} %get-tuple-element.10.high_ref, bf16[1,128,4096]{2,1,0:T(8,128)(2,1)} %get-tuple-element.11.low_ref, f32[1,1,4096]{2,1,0:T(1,128)} %get-tuple-element.12.norm_ref), custom_call_target="tpu_custom_call" | custom-call | tf_op jit(solution)/shard_map/pallas_call | solution.py:437

commit v2 on v1

--- a/solution.py
+++ b/solution.py
@@ -22,7 +22,7 @@
 FAST_LOW = 1.0 / 36
 FAST_STEPS = 7
 FAST_COARSE = 4
-FAST_MISS = 3e-8
+FAST_MISS = 2e-4
 
 
 def cubic_schedule(low, steps):
@@ -97,6 +97,9 @@
     incoming,
     same,
     cross,
+    high_made,
+    low_made,
+    store_sem,
     x_send,
     x_recv,
     w_send,
@@ -127,7 +130,9 @@
             barrier, inc=1, device_id=(lax.rem(beam + j, n_beam), grp), device_id_type=MESH
         )
 
-    held[grp] = jnp.concatenate([data_ref[0], data_ref[1]], axis=1)
+    for w in range(windows):
+        columns = slice(w * width, (w + 1) * width)
+        held[grp, w] = jnp.concatenate([data_ref[0, :, columns], data_ref[1, :, columns]], axis=0)
     entry = lax.broadcasted_iota(jnp.int32, (n_beam, padded, width), 0) * padded + (
         lax.broadcasted_iota(jnp.int32, (n_beam, padded, width), 1)
     )
@@ -145,10 +150,9 @@
 
     def hop(way, step, w):
         source = grp - (step - 1) if way == 0 else grp + (step - 1)
-        rows = pl.ds(w * width, width)
         return pltpu.make_async_remote_copy(
-            src_ref=held.at[source, rows],
-            dst_ref=held.at[source, rows],
+            src_ref=held.at[source, w],
+            dst_ref=held.at[source, w],
             send_sem=x_send.at[way, step - 1, w],
             recv_sem=x_recv.at[way, step - 1, w],
             device_id=(beam, grp + 1 if way == 0 else grp - 1),
@@ -157,10 +161,9 @@
 
     def arrival(way, step, w):
         source = grp - step if way == 0 else grp + step
-        rows = pl.ds(w * width, width)
         return pltpu.make_async_remote_copy(
-            src_ref=held.at[source, rows],
-            dst_ref=held.at[source, rows],
+            src_ref=held.at[source, w],
+            dst_ref=held.at[source, w],
             send_sem=x_send.at[way, step - 1, w],
             recv_sem=x_recv.at[way, step - 1, w],
             device_id=(beam, grp - 1 if way == 0 else grp + 1),
@@ -198,17 +201,12 @@
 
     row = lax.broadcasted_iota(jnp.int32, (width, width), 0)
     col = lax.broadcasted_iota(jnp.int32, (width, width), 1)
-    lanes = held.shape[2]
-    from_lane = lax.broadcasted_iota(jnp.int32, (lanes, lanes), 0)
-    to_lane = lax.broadcasted_iota(jnp.int32, (lanes, lanes), 1)
-    turn = jnp.where(
-        from_lane == to_lane + lanes // 2, -1.0, jnp.where(to_lane == from_lane + lanes // 2, 1.0, 0.0)
-    ).astype(jnp.bfloat16)
+    half = held.shape[2] // 2
 
     def grams(source, w):
-        piece = held[source, w * width : (w + 1) * width, :]
-        turned = plain(piece, turn).astype(jnp.bfloat16)
-        return dot_nt(piece, piece), dot_nt(piece, turned)
+        piece = held[source, w]
+        turned = jnp.concatenate([-piece[half:], piece[:half]], axis=0)
+        return plain(piece, piece, 0), plain(piece, turned, 0)
 
     for w in range(windows):
         same[w], cross[w] = grams(grp, w)
@@ -226,12 +224,11 @@
                     def _():
                         hop(way, step + 1, w).start()
 
-        for way in range(2):
-
-            @pl.when(receives(way, step))
-            def _():
-                source = grp - step if way == 0 else grp + step
-                for w in range(windows):
+            for way in range(2):
+
+                @pl.when(receives(way, step))
+                def _():
+                    source = grp - step if way == 0 else grp + step
                     more_same, more_cross = grams(source, w)
                     same[w] += more_same
                     cross[w] += more_cross
@@ -282,15 +279,23 @@
                 1.0 + sq * (-1.0 / 6 + sq * (1.0 / 120 + sq * (-1.0 / 5040 + sq * (1.0 / 362880))))
             )
             steer = OVERSAMPLE / sine
-            high_ref[u, :, span], low_ref[u, :, span] = halves(steer)
+            high_made[u, :, span], low_made[u, :, span] = halves(steer)
             norm_ref[u, :, span] = jnp.sum(steer * steer, axis=0, keepdims=True)
 
+    stored = [
+        pltpu.make_async_copy(high_made, high_ref, store_sem.at[0]),
+        pltpu.make_async_copy(low_made, low_ref, store_sem.at[1]),
+    ]
+    for copy in stored:
+        copy.start()
     for j in range(1, n_beam):
         o_copies[j - 1].wait_recv()
         for u in range(users):
             out_ref[u] += incoming[j - 1, u]
     for copy in w_copies + o_copies:
         copy.wait_send()
+    for copy in stored:
+        copy.wait()
     for way in range(2):
         for step in range(1, n_grp):
 
@@ -301,7 +306,7 @@
 
 
 def exchange(beam_data, counts, owners, slot_window, grid_index, n_beam, n_grp):
-    rows = beam_data.shape[1]
+    rows = beam_data.shape[2]
     windows = rows // WIN_BEAMS
     padded = -(-windows // 8) * 8
     users, points = grid_index.shape[0], grid_index.shape[2]
@@ -310,6 +315,7 @@
     shares = (users, padded, width)
     vmem = pl.BlockSpec(memory_space=pltpu.VMEM)
     smem = pl.BlockSpec(memory_space=pltpu.SMEM)
+    anywhere = pl.BlockSpec(memory_space=pl.ANY)
     return pl.pallas_call(
         functools.partial(exchange_kernel, n_beam, n_grp, windows, rows * n_beam),
         out_shape=[
@@ -319,15 +325,18 @@
             jax.ShapeDtypeStruct((users, 1, points), jnp.float32),
         ],
         in_specs=[vmem, smem, smem, smem, vmem],
-        out_specs=[vmem] * 4,
+        out_specs=[vmem, anywhere, anywhere, vmem],
         scratch_shapes=[
-            pltpu.VMEM((n_grp, rows, 2 * beam_data.shape[2]), jnp.bfloat16),
+            pltpu.VMEM((n_grp, windows, 2 * beam_data.shape[1], width), jnp.bfloat16),
             pltpu.VMEM((n_beam,) + shares, jnp.float32),
             pltpu.VMEM((n_beam - 1,) + shares, jnp.float32),
             pltpu.VMEM((n_beam - 1,) + sums, jnp.float32),
             pltpu.VMEM((n_beam - 1,) + sums, jnp.float32),
             pltpu.VMEM((windows, width, width), jnp.float32),
             pltpu.VMEM((windows, width, width), jnp.float32),
+            pltpu.VMEM((users, width, points), jnp.bfloat16),
+            pltpu.VMEM((users, width, points), jnp.bfloat16),
+            pltpu.SemaphoreType.DMA((2,)),
             pltpu.SemaphoreType.DMA((2, n_grp - 1, windows)),
             pltpu.SemaphoreType.DMA((2, n_grp - 1, windows)),
             pltpu.SemaphoreType.DMA((n_beam - 1,)),
@@ -340,14 +349,21 @@
 
 
 def spectrum_kernel(
-    beams_total, sum_ref, count_ref, high_ref, low_ref, norm_ref, out_ref, basis_ref
+    beams_total, sum_ref, count_ref, high_ref, low_ref, norm_ref, out_ref, basis_ref, high, low, load_sem
 ):
+    user = pl.program_id(0)
+    loads = [
+        pltpu.make_async_copy(high_ref.at[user], high, load_sem.at[0]),
+        pltpu.make_async_copy(low_ref.at[user], low, load_sem.at[1]),
+    ]
+    for copy in loads:
+        copy.start()
     width, dim = WIN_BEAMS, NOISE_DIM
     packed = sum_ref[0]
     flipped = packed.T
     row = lax.broadcasted_iota(jnp.int32, (width, width), 0)
     col = lax.broadcasted_iota(jnp.int32, (width, width), 1)
-    count = count_ref[pl.program_id(0)].astype(jnp.float32)
+    count = count_ref[user].astype(jnp.float32)
     inverse_count = 1.0 / (jnp.zeros((1, width), jnp.float32) + count * SNAPS)
     real_sum = jnp.where(col >= row, packed, flipped) * inverse_count
     imag_sum = jnp.where(col < row, packed, jnp.where(col > row, -flipped, 0.0)) * inverse_count
@@ -393,10 +409,24 @@
         elif step > 0:
             gram = plain(parts[0], parts[0], 0)
         block = a * block - b * dot3(parts, halves(gram))
-    basis_ref[...] = block
-    parts = halves(block)
-    miss = dot3(parts, parts, 0) - eye
+    miss = gram - eye
     well = jnp.sum(miss * miss) < FAST_MISS
+
+    def put(basis):
+        theta = row.astype(jnp.float32) * (math.pi / beams_total)
+        weight = basis[:width] * jnp.cos(theta) + basis[width:] * jnp.sin(theta)
+        weight = halves(weight.T)
+        points = norm_ref.shape[-1]
+        chunk = math.gcd(CHUNK, points)
+        for at in range(0, points, chunk):
+            span = slice(at, at + chunk)
+            projected = dot3(weight, (high[:, span], low[:, span]))
+            leakage = jnp.sum(projected * projected, axis=0, keepdims=True) / norm_ref[0, :, span]
+            out_ref[0, :, span] = 1.0 / (leakage + spectral_floor)
+
+    for copy in loads:
+        copy.wait()
+    put(block)
 
     @pl.when(jnp.logical_not(well))
     def _():
@@ -414,18 +444,7 @@
             basis_ref[...] = cubic(dot(second, basis_ref[...]), pairs)
 
         basis_ref[...] = cubic(basis_ref[...], [(1.5, 0.5)] * 4)
-
-    theta = row.astype(jnp.float32) * (math.pi / beams_total)
-    weight = basis_ref[:width, :] * jnp.cos(theta) + basis_ref[width:, :] * jnp.sin(theta)
-    weight = weight.T
-    weight = halves(weight)
-    points = norm_ref.shape[-1]
-    chunk = math.gcd(CHUNK, points)
-    for at in range(0, points, chunk):
-        span = slice(at, at + chunk)
-        projected = dot3(weight, (high_ref[0, :, span], low_ref[0, :, span]))
-        leakage = jnp.sum(projected * projected, axis=0, keepdims=True) / norm_ref[0, :, span]
-        out_ref[0, :, span] = 1.0 / (leakage + spectral_floor)
+        put(basis_ref[...])
 
 
 def finish_users(sums, counts, high, low, norm, beams_total):
@@ -441,19 +460,24 @@
         in_specs=[
             block(width, width),
             pl.BlockSpec(memory_space=pltpu.SMEM),
-            block(width, points),
-            block(width, points),
+            pl.BlockSpec(memory_space=pl.ANY),
+            pl.BlockSpec(memory_space=pl.ANY),
             block(1, points),
         ],
         out_specs=block(1, points),
-        scratch_shapes=[pltpu.VMEM((2 * width, 2 * NOISE_DIM), jnp.float32)],
+        scratch_shapes=[
+            pltpu.VMEM((2 * width, 2 * NOISE_DIM), jnp.float32),
+            pltpu.VMEM((width, points), jnp.bfloat16),
+            pltpu.VMEM((width, points), jnp.bfloat16),
+            pltpu.SemaphoreType.DMA((2,)),
+        ],
     )(sums, counts, high, low, norm).reshape(users, points)
 
 
 def local(n_beam, n_grp, beam_data, window_count, slot_owner, slot_window, grid_index):
     users, points = grid_index.shape
     sums, high, low, norm = exchange(
-        beam_data,
+        jnp.swapaxes(beam_data, 1, 2),
         window_count,
         slot_owner[:, :, 0],
         slot_window,

time: 37.4 us -> 33.5 us (0.90)
  Pallas kernels: 34.8 us -> 32.7 us
  local copies, waits for them, and re-layouts: 1.78 us -> 0 us
    unnamed x1 -> x0, local copies, waits for them, and re-layouts: 1.78 us -> none
    pallas_call x1, Pallas kernels: 9.02 us -> 7.91 us  [finish_users(): pl.pallas_call(functools.partial(spectrum_kernel, beams_total), grid=(use...]
    pallas_call x1, Pallas kernels: 25.8 us -> 24.8 us  [exchange(): pl.pallas_call(functools.partial(exchange_kernel, n_beam, n_grp, windows,...]
where the time goes in v2:
time: 33.5 us; the launch traced here: 33.3 us
  Pallas kernels  32.7 us (98%)
  between operations  0.66 us (2%)
    pallas_call x1, Pallas kernels, exchange(): pl.pallas_call(functools.partial(exchange_kernel, n_beam, n_grp, windows,...  24.8 us
    pallas_call x1, Pallas kernels, finish_users(): pl.pallas_call(functools.partial(spectrum_kernel, beams_total), grid=(use...  7.91 us

profile of v2, /device:TPU:0, one launch (start us, length us, event | category | flops | bytes accessed | tf_op | source)
XLA Modules:
  0.0 33.3 jit_solution(15884766282689495585)
XLA Ops:
  0.7 24.8 %shard_map.55 = (f32[1,128,128]{2,1,0:T(8,128)}, bf16[1,128,4096]{2,1,0:T(8,128)(2,1)}, bf16[1,128,4096]{2,1,0:T(8,128)(2,1)}, f32[1,1,4096]{2,1,0:T(1,128)}) custom-call(bf16[2,64,512]{2,1,0:T(8,128)(2,1)} %bitcast.4, s32[1]{0:T(128)S(6)} %copy.6.count_ref, s32[1,8]{1,0:T(1,128)} %bitcast.6, s32[1,8]{1,0:T(1,128)} %window_ref.1, s32[1,1,4096]{2,1,0:T(1,128)} %bitcast.5), custom_call_target="tpu_custom_call" | custom-call | tf_op jit(solution)/shard_map/pallas_call | solution.py:319
  25.4 7.9 %shard_map.56 = f32[1,1,4096]{2,1,0:T(1,128)} custom-call(f32[1,128,128]{2,1,0:T(8,128)} %get-tuple-element.9.sum_ref, s32[1]{0:T(128)S(6)} %copy.6.count_ref, bf16[1,128,4096]{2,1,0:T(8,128)(2,1)} %get-tuple-element.10.high_ref, bf16[1,128,4096]{2,1,0:T(8,128)(2,1)} %get-tuple-element.11.low_ref, f32[1,1,4096]{2,1,0:T(1,128)} %get-tuple-element.12.norm_ref), custom_call_target="tpu_custom_call" | custom-call | tf_op jit(solution)/shard_map/pallas_call | solution.py:456

commit v3 on v2

--- a/solution.py
+++ b/solution.py
@@ -93,6 +93,8 @@
     held,
     weights,
     weights_in,
+    passing,
+    passed,
     outgoing,
     incoming,
     same,
@@ -104,6 +106,8 @@
     x_recv,
     w_send,
     w_recv,
+    p_send,
+    p_recv,
     o_send,
     o_recv,
 ):
@@ -242,27 +246,60 @@
             total = total + same[w] * shares[u, w : w + 1, :]
         return total
 
-    o_copies = []
-    for j in range(1, n_beam):
-        o_copies.append(
-            pltpu.make_async_remote_copy(
-                src_ref=outgoing.at[j - 1],
-                dst_ref=incoming.at[j - 1],
-                send_sem=o_send.at[j - 1],
-                recv_sem=o_recv.at[j - 1],
-                device_id=(lax.rem(beam + n_beam - j, n_beam), grp),
-                device_id_type=MESH,
-            )
-        )
-    for j in range(1, n_beam):
-        w_copies[j - 1].wait_recv()
+    side = lax.rem(beam, 2)
+    chip = lax.div(beam, 2)
+    chips = n_beam // 2
+    p_copies = [
+        pltpu.make_async_remote_copy(
+            src_ref=passing.at[i],
+            dst_ref=passed.at[i],
+            send_sem=p_send.at[i],
+            recv_sem=p_recv.at[i],
+            device_id=(beam + 1 - 2 * side, grp),
+            device_id_type=MESH,
+        )
+        for i in range(chips)
+    ]
+    o_copies = [
+        pltpu.make_async_remote_copy(
+            src_ref=outgoing.at[i - 1],
+            dst_ref=incoming.at[i - 1],
+            send_sem=o_send.at[i - 1],
+            recv_sem=o_recv.at[i - 1],
+            device_id=(2 * lax.rem(chip + chips - i, chips) + side, grp),
+            device_id_type=MESH,
+        )
+        for i in range(1, chips)
+    ]
+    for copy in w_copies:
+        copy.wait_recv()
+    order = list(range(1, chips)) + [0]
+    for at, i in enumerate(order):
+        shares = weights_in[lax.rem(2 * i + 2 * side + n_beam - 1, n_beam) - 1]
         for u in range(users):
-            outgoing[j - 1, u] = mixed(weights_in[j - 1], u)
-        if j > 1:
-            o_copies[j - 2].start()
+            passing[i, u] = mixed(shares, u)
+        if at > 0:
+            p_copies[order[at - 1]].start()
+    for i in range(1, chips):
+        for u in range(users):
+            outgoing[i - 1, u] = mixed(weights_in[2 * i - 1], u)
+        if i == 1:
+            p_copies[order[-1]].start()
     for u in range(users):
         out_ref[u] = mixed(weights[beam], u)
-    o_copies[-1].start()
+    if chips == 1:
+        p_copies[0].start()
+    for i in range(1, chips):
+        p_copies[i].wait_recv()
+        for u in range(users):
+            outgoing[i - 1, u] += passed[i, u]
+        if i > 1:
+            o_copies[i - 2].start()
+    p_copies[0].wait_recv()
+    for u in range(users):
+        out_ref[u] += passed[0, u]
+    if chips > 1:
+        o_copies[-1].start()
 
     points = grid_ref.shape[-1]
     chunk = math.gcd(CHUNK, points)
@@ -288,11 +325,11 @@
     ]
     for copy in stored:
         copy.start()
-    for j in range(1, n_beam):
-        o_copies[j - 1].wait_recv()
+    for i in range(1, chips):
+        o_copies[i - 1].wait_recv()
         for u in range(users):
-            out_ref[u] += incoming[j - 1, u]
-    for copy in w_copies + o_copies:
+            out_ref[u] += incoming[i - 1, u]
+    for copy in w_copies + p_copies + o_copies:
         copy.wait_send()
     for copy in stored:
         copy.wait()
@@ -330,8 +367,10 @@
             pltpu.VMEM((n_grp, windows, 2 * beam_data.shape[1], width), jnp.bfloat16),
             pltpu.VMEM((n_beam,) + shares, jnp.float32),
             pltpu.VMEM((n_beam - 1,) + shares, jnp.float32),
-            pltpu.VMEM((n_beam - 1,) + sums, jnp.float32),
-            pltpu.VMEM((n_beam - 1,) + sums, jnp.float32),
+            pltpu.VMEM((n_beam // 2,) + sums, jnp.float32),
+            pltpu.VMEM((n_beam // 2,) + sums, jnp.float32),
+            pltpu.VMEM((n_beam // 2 - 1,) + sums, jnp.float32),
+            pltpu.VMEM((n_beam // 2 - 1,) + sums, jnp.float32),
             pltpu.VMEM((windows, width, width), jnp.float32),
             pltpu.VMEM((windows, width, width), jnp.float32),
             pltpu.VMEM((users, width, points), jnp.bfloat16),
@@ -341,8 +380,10 @@
             pltpu.SemaphoreType.DMA((2, n_grp - 1, windows)),
             pltpu.SemaphoreType.DMA((n_beam - 1,)),
             pltpu.SemaphoreType.DMA((n_beam - 1,)),
-            pltpu.SemaphoreType.DMA((n_beam - 1,)),
-            pltpu.SemaphoreType.DMA((n_beam - 1,)),
+            pltpu.SemaphoreType.DMA((n_beam // 2,)),
+            pltpu.SemaphoreType.DMA((n_beam // 2,)),
+            pltpu.SemaphoreType.DMA((n_beam // 2 - 1,)),
+            pltpu.SemaphoreType.DMA((n_beam // 2 - 1,)),
         ],
         compiler_params=pltpu.CompilerParams(collective_id=0, has_side_effects=True),
     )(beam_data, counts, owners, slot_window, grid_index)
@@ -375,13 +416,17 @@
         axis=0,
     )
     parts = halves(covariance)
-    square = halves(dot3(parts, parts))
+    squared = dot3(parts, parts)
+    square = halves(squared)
     fourth = dot3(square, [half[:, :width] for half in square])
     energy = 2.0 * jnp.sum(fourth * fourth, keepdims=True)
     shift_value = shift_factor * jnp.sqrt(jnp.sqrt(jnp.sqrt(energy)))
     row2 = lax.broadcasted_iota(jnp.int32, (2 * width, 2 * width), 0)
     col2 = lax.broadcasted_iota(jnp.int32, (2 * width, 2 * width), 1)
-    shifted = jnp.where(row2 == col2, 1.0, 0.0) - covariance * (1.0 / shift_value)
+    eye2 = jnp.where(row2 == col2, 1.0, 0.0)
+    by_shift = 1.0 / shift_value
+    reduced = covariance * by_shift
+    shifted = eye2 - reduced
 
     def chosen(matrix):
         return jnp.concatenate([matrix[:, :dim], matrix[:, width : width + dim]], axis=1)
@@ -394,8 +439,7 @@
             block = dot(block, a * eye - b * gram)
         return block
 
-    parts = halves(shifted)
-    second = halves(dot3(parts, parts))
+    second = halves((shifted - reduced) + squared * by_shift * by_shift)
     power = dot3(second, second)
     block = dot3(halves(power), halves(chosen(power)))
     parts = halves(block)

time: 33.5 us -> 32 us (0.955)
  Pallas kernels: 32.7 us -> 31.2 us
    pallas_call x1, Pallas kernels: 24.8 us -> 23.4 us  [exchange(): pl.pallas_call(functools.partial(exchange_kernel, n_beam, n_grp, windows,...]
where the time goes in v3:
time: 32 us; the launch traced here: 31.8 us
  Pallas kernels  31.2 us (98%)
  between operations  0.66 us (2%)
    pallas_call x1, Pallas kernels, exchange(): pl.pallas_call(functools.partial(exchange_kernel, n_beam, n_grp, windows,...  23.4 us
    pallas_call x1, Pallas kernels, finish_users(): pl.pallas_call(functools.partial(spectrum_kernel, beams_total), grid=(use...  7.72 us

profile of v3, /device:TPU:0, one launch (start us, length us, event | category | flops | bytes accessed | tf_op | source)
XLA Modules:
  0.0 31.8 jit_solution(2568005921219462095)
XLA Ops:
  0.7 23.4 %shard_map.55 = (f32[1,128,128]{2,1,0:T(8,128)}, bf16[1,128,4096]{2,1,0:T(8,128)(2,1)}, bf16[1,128,4096]{2,1,0:T(8,128)(2,1)}, f32[1,1,4096]{2,1,0:T(1,128)}) custom-call(bf16[2,64,512]{2,1,0:T(8,128)(2,1)} %bitcast.4, s32[1]{0:T(128)S(6)} %copy.6.count_ref, s32[1,8]{1,0:T(1,128)} %bitcast.6, s32[1,8]{1,0:T(1,128)} %window_ref.1, s32[1,1,4096]{2,1,0:T(1,128)} %bitcast.5), custom_call_target="tpu_custom_call" | custom-call | tf_op jit(solution)/shard_map/pallas_call | solution.py:356
  24.1 7.7 %shard_map.56 = f32[1,1,4096]{2,1,0:T(1,128)} custom-call(f32[1,128,128]{2,1,0:T(8,128)} %get-tuple-element.9.sum_ref, s32[1]{0:T(128)S(6)} %copy.6.count_ref, bf16[1,128,4096]{2,1,0:T(8,128)(2,1)} %get-tuple-element.10.high_ref, bf16[1,128,4096]{2,1,0:T(8,128)(2,1)} %get-tuple-element.11.low_ref, f32[1,1,4096]{2,1,0:T(1,128)} %get-tuple-element.12.norm_ref), custom_call_target="tpu_custom_call" | custom-call | tf_op jit(solution)/shard_map/pallas_call | solution.py:500

commit v4 on v3

--- a/solution.py
+++ b/solution.py
@@ -65,6 +65,12 @@
 
 def dot3(left, right, contract=1):
     (left_high, left_low), (right_high, right_low) = left, right
+    if contract == 1 and left_high.shape[1] <= 128:
+        both = plain(
+            jnp.concatenate([left_high, left_low], axis=1),
+            jnp.concatenate([right_high, right_high], axis=0),
+        )
+        return both + plain(left_high, right_low)
     return plain(left_high, right_high, contract) + (
         plain(left_high, right_low, contract) + plain(left_low, right_high, contract)
     )
@@ -446,20 +452,25 @@
     gram = dot3(parts, parts, 0)
     scale = 2.0**0.25 * lax.rsqrt(jnp.sqrt(jnp.sum(gram * gram, keepdims=True)))
     block, gram = block * scale, gram * (scale * scale)
-    for step, (a, b) in enumerate(cubic_schedule(FAST_LOW, FAST_STEPS)):
+    pairs = cubic_schedule(FAST_LOW, FAST_STEPS)
+    for step, (a, b) in enumerate(pairs[:-1]):
         parts = halves(block)
         if step >= FAST_COARSE:
             gram = dot3(parts, parts, 0)
         elif step > 0:
             gram = plain(parts[0], parts[0], 0)
         block = a * block - b * dot3(parts, halves(gram))
+    parts = halves(block)
+    gram = dot3(parts, parts, 0)
     miss = gram - eye
     well = jnp.sum(miss * miss) < FAST_MISS
 
-    def put(basis):
+    def folded(basis):
         theta = row.astype(jnp.float32) * (math.pi / beams_total)
-        weight = basis[:width] * jnp.cos(theta) + basis[width:] * jnp.sin(theta)
-        weight = halves(weight.T)
+        return (basis[:width] * jnp.cos(theta) + basis[width:] * jnp.sin(theta)).T
+
+    def put(weight):
+        weight = halves(weight)
         points = norm_ref.shape[-1]
         chunk = math.gcd(CHUNK, points)
         for at in range(0, points, chunk):
@@ -470,7 +481,9 @@
 
     for copy in loads:
         copy.wait()
-    put(block)
+    last_a, last_b = pairs[-1]
+    weight = folded(block)
+    put(last_a * weight - last_b * dot3(halves(gram), halves(weight)))
 
     @pl.when(jnp.logical_not(well))
     def _():
@@ -488,7 +501,7 @@
             basis_ref[...] = cubic(dot(second, basis_ref[...]), pairs)
 
         basis_ref[...] = cubic(basis_ref[...], [(1.5, 0.5)] * 4)
-        put(basis_ref[...])
+        put(folded(basis_ref[...]))
 
 
 def finish_users(sums, counts, high, low, norm, beams_total):

time: 32 us -> 31.7 us (level)
  Pallas kernels: 31.2 us -> 30.8 us
    pallas_call x1, Pallas kernels: 7.72 us -> 7.36 us  [finish_users(): pl.pallas_call(functools.partial(spectrum_kernel, beams_total), grid=(use...]
where the time goes in v4:
time: 31.7 us; the launch traced here: 31.5 us
  Pallas kernels  30.8 us (97%)
  between operations  0.66 us (2%)
    pallas_call x1, Pallas kernels, exchange(): pl.pallas_call(functools.partial(exchange_kernel, n_beam, n_grp, windows,...  23.4 us
    pallas_call x1, Pallas kernels, finish_users(): pl.pallas_call(functools.partial(spectrum_kernel, beams_total), grid=(use...  7.36 us

profile of v4, /device:TPU:0, one launch (start us, length us, event | category | flops | bytes accessed | tf_op | source)
XLA Modules:
  0.0 31.5 jit_solution(8900599786472804212)
XLA Ops:
  0.7 23.4 %shard_map.55 = (f32[1,128,128]{2,1,0:T(8,128)}, bf16[1,128,4096]{2,1,0:T(8,128)(2,1)}, bf16[1,128,4096]{2,1,0:T(8,128)(2,1)}, f32[1,1,4096]{2,1,0:T(1,128)}) custom-call(bf16[2,64,512]{2,1,0:T(8,128)(2,1)} %bitcast.4, s32[1]{0:T(128)S(6)} %copy.6.count_ref, s32[1,8]{1,0:T(1,128)} %bitcast.6, s32[1,8]{1,0:T(1,128)} %window_ref.1, s32[1,1,4096]{2,1,0:T(1,128)} %bitcast.5), custom_call_target="tpu_custom_call" | custom-call | tf_op jit(solution)/shard_map/pallas_call | solution.py:362
  24.1 7.4 %shard_map.56 = f32[1,1,4096]{2,1,0:T(1,128)} custom-call(f32[1,128,128]{2,1,0:T(8,128)} %get-tuple-element.9.sum_ref, s32[1]{0:T(128)S(6)} %copy.6.count_ref, bf16[1,128,4096]{2,1,0:T(8,128)(2,1)} %get-tuple-element.10.high_ref, bf16[1,128,4096]{2,1,0:T(8,128)(2,1)} %get-tuple-element.11.low_ref, f32[1,1,4096]{2,1,0:T(1,128)} %get-tuple-element.12.norm_ref), custom_call_target="tpu_custom_call" | custom-call | tf_op jit(solution)/shard_map/pallas_call | solution.py:513
